TPU v7x, 16 devices: a 4x2x1 block of a 4x4x8 slice. The times are simulated.
16 devices in a mesh: dp: 2 (over y, z), tp: 8 (over x, core).
Axes of the slice: x: 4, y: 2, z: 1, core: 2. Of those that a mesh axis runs over, the one named last changes fastest.
The devices are a block of a 4x4x8 slice.
Arguments:
- x: bfloat16 [4096, 4096], P(('dp', 'tp')), parts along dimension 0
- dy: bfloat16 [4096, 4096], P(('dp', 'tp')), parts along dimension 0
- gate: bfloat16 [4096, 16384], P('dp', 'tp'), parts along dimension 0
- up: bfloat16 [4096, 16384], P('dp', 'tp'), parts along dimension 0
- w_gate: bfloat16 [4096, 16384], P(None, 'tp')
- w_up: bfloat16 [4096, 16384], P(None, 'tp')
- w_down: bfloat16 [16384, 4096], P('tp')
Outputs:
- output 1: bfloat16 [4096, 4096], P(('dp', 'tp')), parts along dimension 0
- output 2: bfloat16 [8192, 16384], P('dp', 'tp'), parts along dimension 0
- output 3: bfloat16 [8192, 16384], P('dp', 'tp'), parts along dimension 0
- output 4: bfloat16 [32768, 4096], P(('dp', 'tp')), parts along dimension 0
There are 2 independent parts. A program takes and returns all parts, laid end to end along the dimension named above; an argument that names none is the same for every part.
All inputs are finite; a program needn't handle non-finite values.
Results may differ from a plain program's by a relative error of at most 0.012.
Values are sent between devices in bfloat16 or wider.
A program may use at most 768 MiB of HBM per device.

v0:
```python
import functools

import jax
import jax.numpy as jnp
from jax import lax
from jax.experimental import pallas as pl
from jax.experimental.pallas import tpu as pltpu
from jax.sharding import PartitionSpec as P

BF16, F32 = jnp.bfloat16, jnp.float32
NT = (((1,), (1,)), ((), ()))
TN = (((0,), (0,)), ((), ()))
VMEM_LIMIT = 67043328
TILE = 1024


def dot(a, b, dims):
    return lax.dot_general(a, b, dims, preferred_element_type=F32)


def gather_kernel(
    chips,
    dy, x, gate, up, w_gate, w_up, w_down,
    dy_all, x_all, d_gate, d_up, hidden, dx_term,
    dy_tile, w_tile, act_tile, grads, hid, dx_tile, x_own,
    send_sem, recv_sem, w_sem, dy_sem, act_sem, grads_sem, hid_sem, dx_sem, own_sem,
):
    rows, width = dy.shape
    half = rows // 2
    ff = w_down.shape[0]
    down_tiles, up_tiles = ff // TILE, width // TILE
    me = lax.axis_index("tp")
    chip, core = me // 2, me % 2
    right, left, far = (chip + 1) % chips, (chip + chips - 1) % chips, (chip + 2) % chips
    to_right, to_left, partner = right * 2 + core, left * 2 + core, chip * 2 + 1 - core

    def span(device, h):
        return pl.ds(pl.multiple_of(device * rows + h * half, half), half)

    plan = [
        (me, 0, True, to_right), (me, 1, True, to_left), (me, 1, True, to_right), (me, 0, True, to_left),
        (me, 0, True, partner), (me, 1, True, partner),
        (to_left, 0, False, to_right), (to_right, 1, False, to_left),
        (to_left, 0, False, partner), (to_right, 1, False, partner),
        (to_left, 1, False, partner), (to_right, 0, False, partner),
        (far * 2 + core, 0, False, partner), (far * 2 + core, 1, False, partner),
    ]

    def remote(which, k):
        mine, whole = ((dy, dy_all), (x, x_all))[which]
        device, h, own, target = plan[k]
        return pltpu.make_async_remote_copy(
            src_ref=mine.at[pl.ds(h * half, half)] if own else whole.at[span(device, h)],
            dst_ref=whole.at[span(device, h)],
            send_sem=send_sem.at[which, k],
            recv_sem=recv_sem.at[which, k],
            device_id={"tp": target},
            device_id_type=pl.DeviceIdType.MESH,
        )

    def send(which, *ks):
        for k in ks:
            remote(which, k).start()

    def arrived(which, *ks):
        for k in ks:
            remote(which, k).wait_recv()

    def piece(s, p):
        near = (left if p < 2 else right) * 2 * rows + (p % 2) * rows
        first = 0 if p < 2 else half
        near = near + jnp.where(s == 1, first, half - first)
        whole = jnp.where(s == 0, chip, far) * 2 * rows + p * half
        start = jnp.where((s == 1) | (s == 2), near, whole)
        return pl.ds(pl.multiple_of(start, half), half)

    def part(p):
        return pl.ds(p * half, half)

    def load_dy(s, slot):
        for p in range(4):
            pltpu.make_async_copy(dy_all.at[piece(s, p)], dy_tile.at[slot, part(p)], dy_sem.at[slot]).start()

    def wait_dy(slot):
        pltpu.make_async_copy(dy_all.at[pl.ds(0, 4 * half)], dy_tile.at[slot], dy_sem.at[slot]).wait()

    def load_act(s):
        for i in range(down_tiles):
            cols = pl.ds(i * TILE, TILE)
            for p in range(4):
                for j, a in enumerate((gate, up)):
                    pltpu.make_async_copy(
                        a.at[piece(s, p), cols], act_tile.at[i, part(p), pl.ds(j * TILE, TILE)], act_sem.at[i]
                    ).start()

    def wait_act(i):
        pltpu.make_async_copy(gate.at[pl.ds(0, 4 * half), pl.ds(0, 2 * TILE)], act_tile.at[i], act_sem.at[i]).wait()

    def load_down(i, slot):
        at = pl.ds(pl.multiple_of(i * TILE, TILE), TILE)
        pltpu.make_async_copy(w_down.at[at], w_tile.at[slot], w_sem.at[slot]).start()

    def load_up(i, slot):
        at = pl.ds(pl.multiple_of(i * TILE, TILE), TILE)
        for j, w in enumerate((w_gate, w_up)):
            pltpu.make_async_copy(w.at[at], w_tile.at[slot, :, pl.ds(j * ff, ff)], w_sem.at[slot]).start()

    def wait_w(slot):
        pltpu.make_async_copy(w_down.at[pl.ds(0, TILE)], w_tile.at[slot], w_sem.at[slot]).wait()

    own_rows = pl.ds(pl.multiple_of(core * rows, rows), rows)
    all_rows = pl.ds(pl.multiple_of(me * rows, rows), rows)
    own_dy_in = pltpu.make_async_copy(dy, dy_tile.at[0, own_rows], own_sem.at[0])
    own_dy_out = pltpu.make_async_copy(dy_tile.at[0, own_rows], dy_all.at[all_rows], own_sem.at[1])
    own_x_in = pltpu.make_async_copy(x, x_own, own_sem.at[2])
    own_x_out = pltpu.make_async_copy(x_own, x_all.at[all_rows], own_sem.at[3])
    partner_rows = pl.ds(pl.multiple_of((1 - core) * rows, rows), rows)
    partner_all = pl.ds(pl.multiple_of(partner * rows, rows), rows)
    partner_dy_in = pltpu.make_async_copy(dy_all.at[partner_all], dy_tile.at[0, partner_rows], own_sem.at[4])

    load_down(0, 0)
    own_dy_in.start()
    load_act(0)
    barrier = pltpu.get_barrier_semaphore()
    for target in (to_right, to_left, partner):
        pl.semaphore_signal(barrier, inc=1, device_id={"tp": target}, device_id_type=pl.DeviceIdType.MESH)
    pl.semaphore_wait(barrier, 3)
    send(0, 4, 5, 0, 1, 2, 3)
    own_x_in.start()
    own_dy_in.wait()
    own_dy_out.start()
    arrived(0, 4, 5)
    partner_dy_in.start()
    partner_dy_in.wait()

    def step(s, _):
        slot_dy = s % 2

        @pl.when(s > 0)
        def _():
            wait_dy(slot_dy)

        def down(i, _):
            wait_w(i)

            @pl.when(i == 0)
            def _():
                load_down(1, 1)

            @pl.when(i == 1)
            def _():
                load_up(0, 0)

            @pl.when((s == 3) & (i == 0))
            def _():
                arrived(1, 0, 1)
                send(1, 6, 7, 8, 9)

            wait_act(i)

            @pl.when((s > 0) & (i == 0))
            def _():
                pltpu.make_async_copy(grads, dy_all.at[pl.ds(0, 4 * half)], grads_sem).wait()
                pltpu.make_async_copy(hid, hidden.at[pl.ds(0, 4 * half)], hid_sem).wait()

            d_hidden = dot(dy_tile[slot_dy], w_tile[i], NT)
            g, u = act_tile[i, :, :TILE].astype(F32), act_tile[i, :, TILE:].astype(F32)
            sig = jax.nn.sigmoid(g)
            act = g * sig
            at = pl.multiple_of(i * TILE, TILE)
            grads[:, pl.ds(at, TILE)] = (d_hidden * u * (sig + act * (1.0 - sig))).astype(BF16)
            grads[:, pl.ds(ff + at, TILE)] = (d_hidden * act).astype(BF16)
            hid[:, pl.ds(at, TILE)] = (act * u).astype(BF16)
            return 0

        lax.fori_loop(0, down_tiles, down, 0)
        for p in range(4):
            to = piece(s, p)
            pltpu.make_async_copy(grads.at[part(p), pl.ds(0, ff)], d_gate.at[to], grads_sem).start()
            pltpu.make_async_copy(grads.at[part(p), pl.ds(ff, ff)], d_up.at[to], grads_sem).start()
            pltpu.make_async_copy(hid.at[part(p)], hidden.at[to], hid_sem).start()

        @pl.when(s < 3)
        def _():
            load_act(s + 1)

        def back(i, _):
            slot = i % 2
            wait_w(slot)

            @pl.when(i < up_tiles - 1)
            def _():
                load_up(i + 1, 1 - slot)

            @pl.when((i == up_tiles - 1) & (s < 3))
            def _():
                load_down(0, 1 - slot)

            @pl.when((s == 0) & (i == 2))
            def _():
                own_x_in.wait()
                own_x_out.start()
                arrived(0, 0, 1)
                send(0, 6, 7, 8, 9)
                send(1, 0, 1, 2, 3, 4, 5)

            @pl.when((s == 0) & (i == 3))
            def _():
                own_dy_out.wait()
                arrived(0, 8, 9)

            @pl.when((s == 1) & (i == 1))
            def _():
                arrived(0, 2, 3)
                send(0, 10, 11)

            @pl.when((s == 1) & (i == 3))
            def _():
                arrived(0, 10, 11)

            @pl.when((s == 2) & (i == 0))
            def _():
                arrived(0, 6, 7)
                send(0, 12, 13)

            @pl.when((s == 2) & (i == 3))
            def _():
                arrived(0, 12, 13)

            @pl.when((s < 3) & (i == 3))
            def _():
                load_dy(s + 1, 1 - slot_dy)

            @pl.when((s == 3) & (i == 2))
            def _():
                arrived(1, 2, 3)
                send(1, 10, 11)

            @pl.when((s > 0) | (i > 1))
            def _():
                wait_dx(slot)

            dx_tile[slot] = dot(grads[...], w_tile[slot], NT).astype(BF16)
            cols = pl.ds(pl.multiple_of(i * TILE, TILE), TILE)
            for p in range(4):
                pltpu.make_async_copy(dx_tile.at[slot, part(p)], dx_term.at[piece(s, p), cols], dx_sem.at[slot]).start()
            return 0

        def wait_dx(slot):
            pltpu.make_async_copy(dx_tile.at[slot], dx_term.at[pl.ds(0, 4 * half), pl.ds(0, TILE)], dx_sem.at[slot]).wait()

        lax.fori_loop(0, up_tiles, back, 0)

        @pl.when(s == 3)
        def _():
            wait_dx(0)
            wait_dx(1)

        return 0

    lax.fori_loop(0, 4, step, 0)
    pltpu.make_async_copy(grads, dy_all.at[pl.ds(0, 4 * half)], grads_sem).wait()
    pltpu.make_async_copy(hid, hidden.at[pl.ds(0, 4 * half)], hid_sem).wait()
    own_x_out.wait()
    arrived(1, 6, 7)
    send(1, 12, 13)
    arrived(1, 4, 5, 8, 9, 10, 11, 12, 13)
    for which in range(2):
        for k in range(len(plan)):
            remote(which, k).wait_send()


def gather_and_back(n, dy, x, gate, up, w_gate, w_up, w_down):
    rows, width = dy.shape
    ff = w_down.shape[0]
    group = rows * n
    any_ = pl.BlockSpec(memory_space=pl.ANY)
    wide = jax.ShapeDtypeStruct((group, width), BF16)
    narrow = jax.ShapeDtypeStruct((group, ff), BF16)
    sem = pltpu.SemaphoreType.DMA
    return pl.pallas_call(
        functools.partial(gather_kernel, n // 2),
        out_shape=[wide, wide, narrow, narrow, narrow, wide],
        in_specs=[any_] * 7,
        out_specs=[any_] * 6,
        scratch_shapes=[
            pltpu.VMEM((2, 2 * rows, width), BF16),
            pltpu.VMEM((2, TILE, width), BF16),
            pltpu.VMEM((2, 2 * rows, 2 * TILE), BF16),
            pltpu.VMEM((2 * rows, 2 * ff), BF16),
            pltpu.VMEM((2 * rows, ff), BF16),
            pltpu.VMEM((2, 2 * rows, TILE), BF16),
            pltpu.VMEM((rows, width), BF16),
            sem((2, 14)), sem((2, 14)), sem((2,)), sem((2,)), sem((2,)), sem, sem, sem((2,)), sem((5,)),
        ],
        compiler_params=pltpu.CompilerParams(collective_id=0, has_side_effects=True, vmem_limit_bytes=VMEM_LIMIT),
        cost_estimate=pl.CostEstimate(flops=6 * group * width * ff, bytes_accessed=16 * group * width, transcendentals=0),
        name="gather_and_back",
    )(dy, x, gate, up, w_gate, w_up, w_down)


def weight_grads(x, d_gate, d_up, hidden, dy, bm=1024, bn=1024):
    tokens, width = x.shape
    ff = d_gate.shape[1]
    nf, nd = ff // bn, width // bn
    first = (ff // bm) * nd
    total = first + (width // bm) * 2 * nf

    def a(t):
        return jnp.minimum(t, first - 1)

    def b(t):
        return jnp.maximum(t - first, 0)

    def gate_col(t):
        return jnp.minimum(b(t) % (2 * nf), nf - 1)

    def up_col(t):
        return jnp.maximum(b(t) % (2 * nf) - nf, 0)

    def kernel(x_ref, dg_ref, du_ref, hid_ref, dy_ref, og_ref, ou_ref, od_ref):
        t = pl.program_id(0)
        r = b(t) % (2 * nf)

        @pl.when(t < first)
        def _():
            od_ref[...] = dot(hid_ref[...], dy_ref[...], TN).astype(BF16)

        @pl.when((t >= first) & (r < nf))
        def _():
            og_ref[...] = dot(x_ref[...], dg_ref[...], TN).astype(BF16)

        @pl.when((t >= first) & (r >= nf))
        def _():
            ou_ref[...] = dot(x_ref[...], du_ref[...], TN).astype(BF16)

    return pl.pallas_call(
        kernel,
        grid=(total,),
        in_specs=[
            pl.BlockSpec((tokens, bm), lambda t: (0, b(t) // (2 * nf))),
            pl.BlockSpec((tokens, bn), lambda t: (0, gate_col(t))),
            pl.BlockSpec((tokens, bn), lambda t: (0, up_col(t))),
            pl.BlockSpec((tokens, bm), lambda t: (0, a(t) // nd)),
            pl.BlockSpec((tokens, bn), lambda t: (0, a(t) % nd)),
        ],
        out_specs=[
            pl.BlockSpec((bm, bn), lambda t: (b(t) // (2 * nf), gate_col(t))),
            pl.BlockSpec((bm, bn), lambda t: (b(t) // (2 * nf), up_col(t))),
            pl.BlockSpec((bm, bn), lambda t: (a(t) // nd, a(t) % nd)),
        ],
        out_shape=[
            jax.ShapeDtypeStruct((width, ff), BF16),
            jax.ShapeDtypeStruct((width, ff), BF16),
            jax.ShapeDtypeStruct((ff, width), BF16),
        ],
        compiler_params=pltpu.CompilerParams(dimension_semantics=("arbitrary",), vmem_limit_bytes=VMEM_LIMIT),
        cost_estimate=pl.CostEstimate(flops=6 * tokens * width * ff, bytes_accessed=16 * tokens * width, transcendentals=0),
        name="weight_grads",
    )(x, d_gate, d_up, hidden, dy)


def solution(mesh):
    n = mesh.shape["tp"]

    def step(x, dy, gate, up, w_gate, w_up, w_down):
        dy_all, x_all, d_gate, d_up, hidden, dx_term = gather_and_back(n, dy, x, gate, up, w_gate, w_up, w_down)
        dx = lax.psum_scatter(dx_term, "tp", scatter_dimension=0, tiled=True)
        dw_gate, dw_up, dw_down = weight_grads(x_all, d_gate, d_up, hidden, dy_all)
        return dx, dw_gate, dw_up, dw_down

    token, feature = P(("dp", "tp"), None), P("dp", "tp")
    return jax.shard_map(
        step,
        mesh=mesh,
        in_specs=(token, token, feature, feature, P(None, "tp"), P(None, "tp"), P("tp", None)),
        out_specs=(token, feature, feature, token),
        check_vma=False,
    )
```

profile of v0, /device:TPU:113, one launch (start us, length us, event | category | flops | bytes accessed | tf_op | source)
XLA Modules:
  0.0 283.3 jit_solution(1253984510337126600)
XLA Ops:
  7.2 0.1 reduce-scatter.2.cloned.1.call-start
  7.2 145.2 %gather_and_back.1 = (bf16[2048,4096]{1,0:T(8,128)(2,1)}, bf16[2048,4096]{1,0:T(8,128)(2,1)}, bf16[2048,2048]{1,0:T(8,128)(2,1)}, bf16[2048,2048]{1,0:T(8,128)(2...) custom-call(bf16[256,4096]{1,0:T(8,128)(2,1)} %dy.1, bf16[256,4096]{1,0:T(8,128)(2,1)} %x.1, ...), custom_call_target="tpu_custom_call" | custom-call | flops 103079215104 | bytes 134217728 | tf_op jit(solution)/shard_map/gather_and_back/pallas_call | solution.py:281
  152.4 0.1 reduce-scatter.2.cloned.1.call-update
  152.5 124.0 %weight_grads.1 = (bf16[4096,2048]{1,0:T(8,128)(2,1)}, bf16[4096,2048]{1,0:T(8,128)(2,1)}, bf16[2048,4096]{1,0:T(8,128)(2,1)}) custom-call(bf16[2048,4096]{1,0:T(8,128)(2,1)} %get-tuple-element.14.x_ref, bf16[2048,2048]{1,0:T(8,128)(2,1)} %get-tuple-element.15.dg_ref, bf16[2048,2048]{1,0:T(8,128)(2,1)} %get-tuple-element.16.du_ref, ...), custom_call_target="tpu_custom_call" | custom-call | flops 103079215104 | bytes 134217728 | tf_op jit(solution)/shard_map/weight_grads/pallas_call | solution.py:337
  276.5 0.0 reduce-scatter.2.cloned.1.call-done
Async XLA Ops:
  7.2 269.3 %reduce-scatter.2.cloned.1.call-start = ((), (), s32[]{:S(2)}) async-start(), calls=%async_computation.1 | async-start | bytes 18874368 | tf_op jit(solution)/shard_map/reduce_scatter | solution.py:368
Sparse Core Ops, SparseCore 0:
  152.6 87.9 reduce-scatter.1
where the time goes:
time: 283 us
  Pallas kernels  269 us (95%)
  between operations  14.1 us (5%)
    pallas_call x1, Pallas kernels, gather_and_back(): pl.pallas_call(functools.partial(gather_kernel, n // 2), out_shape=[wide,...  145 us
    pallas_call x1, Pallas kernels, weight_grads(): pl.pallas_call(kernel, grid=(total,), in_specs=[pl.BlockSpec((tokens, bm)...  124 us
  transfers between devices with their start and end apart: 1, of which 0 were waited for; matrix products, arithmetic and copies ran while one was open for 0% of the time, Pallas kernels for 44%

commit v1 on v0

--- a/solution.py
+++ b/solution.py
@@ -21,9 +21,9 @@
 def gather_kernel(
     chips,
     dy, x, gate, up, w_gate, w_up, w_down,
-    dy_all, x_all, d_gate, d_up, hidden, dx_term,
-    dy_tile, w_tile, act_tile, grads, hid, dx_tile, x_own,
-    send_sem, recv_sem, w_sem, dy_sem, act_sem, grads_sem, hid_sem, dx_sem, own_sem,
+    dy_all, x_all, d_gate, d_up, hidden, dx_term, corner,
+    dy_tile, w_tile, act_tile, grads, hid, dx_tile, x_own, corner_left, corner_right,
+    send_sem, recv_sem, w_sem, dy_sem, act_sem, grads_sem, hid_sem, dx_sem, own_sem, corner_sem,
 ):
     rows, width = dy.shape
     half = rows // 2
@@ -108,6 +108,11 @@
     def wait_w(slot):
         pltpu.make_async_copy(w_down.at[pl.ds(0, TILE)], w_tile.at[slot], w_sem.at[slot]).wait()
 
+    def corner_in(k):
+        if k == 0:
+            return pltpu.make_async_copy(hidden.at[:, pl.ds(0, TILE)], corner_left, corner_sem.at[0])
+        return pltpu.make_async_copy(dy_all.at[:, pl.ds((k - 1) * TILE, TILE)], corner_right.at[k - 1], corner_sem.at[k])
+
     own_rows = pl.ds(pl.multiple_of(core * rows, rows), rows)
     all_rows = pl.ds(pl.multiple_of(me * rows, rows), rows)
     own_dy_in = pltpu.make_async_copy(dy, dy_tile.at[0, own_rows], own_sem.at[0])
@@ -118,14 +123,14 @@
     partner_all = pl.ds(pl.multiple_of(partner * rows, rows), rows)
     partner_dy_in = pltpu.make_async_copy(dy_all.at[partner_all], dy_tile.at[0, partner_rows], own_sem.at[4])
 
-    load_down(0, 0)
-    own_dy_in.start()
-    load_act(0)
     barrier = pltpu.get_barrier_semaphore()
     for target in (to_right, to_left, partner):
         pl.semaphore_signal(barrier, inc=1, device_id={"tp": target}, device_id_type=pl.DeviceIdType.MESH)
+    load_down(0, 0)
+    own_dy_in.start()
     pl.semaphore_wait(barrier, 3)
-    send(0, 4, 5, 0, 1, 2, 3)
+    send(0, 0, 1, 4, 5, 2, 3)
+    load_act(0)
     own_x_in.start()
     own_dy_in.wait()
     own_dy_out.start()
@@ -235,6 +240,9 @@
             def _():
                 arrived(1, 2, 3)
                 send(1, 10, 11)
+                pltpu.make_async_copy(hid, hidden.at[pl.ds(0, 4 * half)], hid_sem).wait()
+                for k in range(3):
+                    corner_in(k).start()
 
             @pl.when((s > 0) | (i > 1))
             def _():
@@ -260,10 +268,28 @@
 
     lax.fori_loop(0, 4, step, 0)
     pltpu.make_async_copy(grads, dy_all.at[pl.ds(0, 4 * half)], grads_sem).wait()
-    pltpu.make_async_copy(hid, hidden.at[pl.ds(0, 4 * half)], hid_sem).wait()
     own_x_out.wait()
-    arrived(1, 6, 7)
-    send(1, 12, 13)
+    corner_in(0).wait()
+
+    def corner_part(k, _):
+        @pl.when(k == 0)
+        def _():
+            corner_in(1).wait()
+
+        @pl.when(k == 1)
+        def _():
+            corner_in(2).wait()
+            arrived(1, 6, 7)
+            send(1, 12, 13)
+
+        cols = pl.ds(pl.multiple_of(k * TILE, TILE), TILE)
+        w_tile[0, :, cols] = dot(corner_left[...], corner_right[k], TN).astype(BF16)
+        return 0
+
+    lax.fori_loop(0, 2, corner_part, 0)
+    corner_out = pltpu.make_async_copy(w_tile.at[0, :, pl.ds(0, 2 * TILE)], corner, corner_sem.at[3])
+    corner_out.start()
+    corner_out.wait()
     arrived(1, 4, 5, 8, 9, 10, 11, 12, 13)
     for which in range(2):
         for k in range(len(plan)):
@@ -280,9 +306,9 @@
     sem = pltpu.SemaphoreType.DMA
     return pl.pallas_call(
         functools.partial(gather_kernel, n // 2),
-        out_shape=[wide, wide, narrow, narrow, narrow, wide],
+        out_shape=[wide, wide, narrow, narrow, narrow, wide, jax.ShapeDtypeStruct((TILE, 2 * TILE), BF16)],
         in_specs=[any_] * 7,
-        out_specs=[any_] * 6,
+        out_specs=[any_] * 7,
         scratch_shapes=[
             pltpu.VMEM((2, 2 * rows, width), BF16),
             pltpu.VMEM((2, TILE, width), BF16),
@@ -291,7 +317,9 @@
             pltpu.VMEM((2 * rows, ff), BF16),
             pltpu.VMEM((2, 2 * rows, TILE), BF16),
             pltpu.VMEM((rows, width), BF16),
-            sem((2, 14)), sem((2, 14)), sem((2,)), sem((2,)), sem((2,)), sem, sem, sem((2,)), sem((5,)),
+            pltpu.VMEM((group, TILE), BF16),
+            pltpu.VMEM((2, group, TILE), BF16),
+            sem((2, 14)), sem((2, 14)), sem((2,)), sem((2,)), sem((2,)), sem, sem, sem((2,)), sem((5,)), sem((4,)),
         ],
         compiler_params=pltpu.CompilerParams(collective_id=0, has_side_effects=True, vmem_limit_bytes=VMEM_LIMIT),
         cost_estimate=pl.CostEstimate(flops=6 * group * width * ff, bytes_accessed=16 * group * width, transcendentals=0),
@@ -299,74 +327,119 @@
     )(dy, x, gate, up, w_gate, w_up, w_down)
 
 
-def weight_grads(x, d_gate, d_up, hidden, dy, bm=1024, bn=1024):
+def choose(t, values):
+    out = values[0]
+    for k in range(1, len(values)):
+        if values[k] != values[k - 1]:
+            out = jnp.where(t >= k, values[k], out)
+    return out
+
+
+def grads_kernel(
+    x, d_gate, d_up, hidden, dy, corner, dw_gate, dw_up, dw_down, lhs, rhs, out, through, lhs_sem, rhs_sem, out_sem, corner_sem
+):
+    bm, bn = lhs.shape[2], rhs.shape[2]
+    lefts = [(hidden, 1, 0), (hidden, 0, 1), (x, 0, 2), (x, 1, 0), (x, 2, 1), (x, 3, 2)]
+    rights = [(dy, 0, 0), (dy, 1, 1), (d_gate, 0, 2), (d_up, 0, 0)]
+    steps = [
+        (0, 0, dw_down, 1, 0), (0, 1, dw_down, 1, 1), (1, 1, dw_down, 0, 1),
+        (2, 2, dw_gate, 0, 0), (2, 3, dw_up, 0, 0), (3, 3, dw_up, 1, 0), (3, 2, dw_gate, 1, 0),
+        (4, 2, dw_gate, 2, 0), (4, 3, dw_up, 2, 0), (5, 3, dw_up, 3, 0), (5, 2, dw_gate, 3, 0),
+    ]
+
+    def left(k):
+        a, c, slot = lefts[k]
+        return pltpu.make_async_copy(a.at[:, pl.ds(c * bm, bm)], lhs.at[slot], lhs_sem.at[slot])
+
+    def right(k):
+        a, c, slot = rights[k]
+        return pltpu.make_async_copy(a.at[:, pl.ds(c * bn, bn)], rhs.at[slot], rhs_sem.at[slot])
+
+    def store(t, slot):
+        _, _, a, r, c = steps[t]
+        return pltpu.make_async_copy(out.at[slot], a.at[pl.ds(r * bm, bm), pl.ds(c * bn, bn)], out_sem.at[slot])
+
+    corner_in = pltpu.make_async_copy(corner, through, corner_sem.at[0])
+    corner_out = pltpu.make_async_copy(through, dw_down.at[pl.ds(0, bm), pl.ds(0, bn)], corner_sem.at[1])
+    starts = {
+        0: [left(1), right(1)], 1: [left(2), right(2), corner_in], 2: [right(3), left(3)], 3: [left(4), corner_out], 5: [left(5)],
+    }
+    waits = {
+        0: [left(0), right(0)], 1: [right(1)], 2: [left(1)], 3: [left(2), right(2), corner_in], 4: [right(3)],
+        5: [left(3)], 7: [left(4)], 9: [left(5)],
+    }
+    left(0).start()
+    right(0).start()
+
+    def step(t, _):
+        for k in range(len(steps)):
+            if k in waits or k in starts:
+
+                @pl.when(t == k)
+                def _(k=k):
+                    for copy in waits.get(k, ()):
+                        copy.wait()
+                    for copy in starts.get(k, ()):
+                        copy.start()
+
+        slot = t % 2
+
+        @pl.when(t >= 2)
+        def _():
+            store(0, slot).wait()
+
+        a = lhs[choose(t, [lefts[k[0]][2] for k in steps])]
+        b = rhs[choose(t, [rights[k[1]][2] for k in steps])]
+        out[slot] = dot(a, b, TN).astype(BF16)
+        for k in range(len(steps)):
+
+            @pl.when(t == k)
+            def _(k=k):
+                store(k, k % 2).start()
+
+        return 0
+
+    lax.fori_loop(0, len(steps), step, 0)
+    store(0, 0).wait()
+    store(0, 1).wait()
+    corner_out.wait()
+
+
+def weight_grads(x, d_gate, d_up, hidden, dy, corner):
     tokens, width = x.shape
     ff = d_gate.shape[1]
-    nf, nd = ff // bn, width // bn
-    first = (ff // bm) * nd
-    total = first + (width // bm) * 2 * nf
-
-    def a(t):
-        return jnp.minimum(t, first - 1)
-
-    def b(t):
-        return jnp.maximum(t - first, 0)
-
-    def gate_col(t):
-        return jnp.minimum(b(t) % (2 * nf), nf - 1)
-
-    def up_col(t):
-        return jnp.maximum(b(t) % (2 * nf) - nf, 0)
-
-    def kernel(x_ref, dg_ref, du_ref, hid_ref, dy_ref, og_ref, ou_ref, od_ref):
-        t = pl.program_id(0)
-        r = b(t) % (2 * nf)
-
-        @pl.when(t < first)
-        def _():
-            od_ref[...] = dot(hid_ref[...], dy_ref[...], TN).astype(BF16)
-
-        @pl.when((t >= first) & (r < nf))
-        def _():
-            og_ref[...] = dot(x_ref[...], dg_ref[...], TN).astype(BF16)
-
-        @pl.when((t >= first) & (r >= nf))
-        def _():
-            ou_ref[...] = dot(x_ref[...], du_ref[...], TN).astype(BF16)
-
+    bm, bn = 1024, 2048
+    any_ = pl.BlockSpec(memory_space=pl.ANY)
+    sem = pltpu.SemaphoreType.DMA
     return pl.pallas_call(
-        kernel,
-        grid=(total,),
-        in_specs=[
-            pl.BlockSpec((tokens, bm), lambda t: (0, b(t) // (2 * nf))),
-            pl.BlockSpec((tokens, bn), lambda t: (0, gate_col(t))),
-            pl.BlockSpec((tokens, bn), lambda t: (0, up_col(t))),
-            pl.BlockSpec((tokens, bm), lambda t: (0, a(t) // nd)),
-            pl.BlockSpec((tokens, bn), lambda t: (0, a(t) % nd)),
-        ],
-        out_specs=[
-            pl.BlockSpec((bm, bn), lambda t: (b(t) // (2 * nf), gate_col(t))),
-            pl.BlockSpec((bm, bn), lambda t: (b(t) // (2 * nf), up_col(t))),
-            pl.BlockSpec((bm, bn), lambda t: (a(t) // nd, a(t) % nd)),
-        ],
+        grads_kernel,
+        in_specs=[any_] * 6,
+        out_specs=[any_] * 3,
         out_shape=[
             jax.ShapeDtypeStruct((width, ff), BF16),
             jax.ShapeDtypeStruct((width, ff), BF16),
             jax.ShapeDtypeStruct((ff, width), BF16),
         ],
-        compiler_params=pltpu.CompilerParams(dimension_semantics=("arbitrary",), vmem_limit_bytes=VMEM_LIMIT),
+        scratch_shapes=[
+            pltpu.VMEM((3, tokens, bm), BF16),
+            pltpu.VMEM((3, tokens, bn), BF16),
+            pltpu.VMEM((2, bm, bn), BF16),
+            pltpu.VMEM((bm, bn), BF16),
+            sem((3,)), sem((3,)), sem((2,)), sem((2,)),
+        ],
+        compiler_params=pltpu.CompilerParams(vmem_limit_bytes=VMEM_LIMIT),
         cost_estimate=pl.CostEstimate(flops=6 * tokens * width * ff, bytes_accessed=16 * tokens * width, transcendentals=0),
         name="weight_grads",
-    )(x, d_gate, d_up, hidden, dy)
+    )(x, d_gate, d_up, hidden, dy, corner)
 
 
 def solution(mesh):
     n = mesh.shape["tp"]
 
     def step(x, dy, gate, up, w_gate, w_up, w_down):
-        dy_all, x_all, d_gate, d_up, hidden, dx_term = gather_and_back(n, dy, x, gate, up, w_gate, w_up, w_down)
+        dy_all, x_all, d_gate, d_up, hidden, dx_term, corner = gather_and_back(n, dy, x, gate, up, w_gate, w_up, w_down)
         dx = lax.psum_scatter(dx_term, "tp", scatter_dimension=0, tiled=True)
-        dw_gate, dw_up, dw_down = weight_grads(x_all, d_gate, d_up, hidden, dy_all)
+        dw_gate, dw_up, dw_down = weight_grads(x_all, d_gate, d_up, hidden, dy_all, corner)
         return dx, dw_gate, dw_up, dw_down
 
     token, feature = P(("dp", "tp"), None), P("dp", "tp")

time: 283 us -> 266 us (0.940)
  Pallas kernels: 269 us -> 252 us
    pallas_call x1, Pallas kernels: 124 us -> 104 us  [weight_grads(): pl.pallas_call(grads_kernel, in_specs=[any_] * 6, out_specs=[any_] * 3, o...]
  transfers between devices with their start and end apart: 1 -> 1, of which waited for: 0 -> 0; matrix products, arithmetic and copies ran while one was open for 0% -> 0% of each run, Pallas kernels for 44% -> 39%
where the time goes in v1:
time: 266 us
  Pallas kernels  252 us (95%)
  between operations  14.1 us (5%)
    pallas_call x1, Pallas kernels, gather_and_back(): pl.pallas_call(functools.partial(gather_kernel, n // 2), out_shape=[wide,...  147 us
    pallas_call x1, Pallas kernels, weight_grads(): pl.pallas_call(grads_kernel, in_specs=[any_] * 6, out_specs=[any_] * 3, o...  104 us
  transfers between devices with their start and end apart: 1, of which 0 were waited for; matrix products, arithmetic and copies ran while one was open for 0% of the time, Pallas kernels for 39%

profile of v1, /device:TPU:113, one launch (start us, length us, event | category | flops | bytes accessed | tf_op | source)
XLA Modules:
  0.0 265.9 jit_solution(13061972625932825739)
XLA Ops:
  7.2 0.1 reduce-scatter.2.cloned.1.call-start
  7.2 147.2 %gather_and_back.1 = (bf16[2048,4096]{1,0:T(8,128)(2,1)}, bf16[2048,4096]{1,0:T(8,128)(2,1)}, bf16[2048,2048]{1,0:T(8,128)(2,1)}, bf16[2048,2048]{1,0:T(8,128)(2...) custom-call(bf16[256,4096]{1,0:T(8,128)(2,1)} %dy.1, ...), custom_call_target="tpu_custom_call" | custom-call | flops 103079215104 | bytes 134217728 | tf_op jit(solution)/shard_map/gather_and_back/pallas_call | solution.py:307
  154.5 0.1 reduce-scatter.2.cloned.1.call-update
  154.5 104.4 %weight_grads.1 = (bf16[4096,2048]{1,0:T(8,128)(2,1)}, bf16[4096,2048]{1,0:T(8,128)(2,1)}, bf16[2048,4096]{1,0:T(8,128)(2,1)}) custom-call(bf16[2048,4096]{1,0:T(8,128)(2,1)} %get-tuple-element.15.x, bf16[2048,2048]{1,0:T(8,128)(2,1)} %get-tuple-element.16.d_gate, bf16[2048,2048]{1,0:T(8,128)(2,1)} %get-tuple-element.17.d_up, ...), custom_call_target="tpu_custom_call" | custom-call | flops 103079215104 | bytes 134217728 | tf_op jit(solution)/shard_map/weight_grads/pallas_call | solution.py:414
  259.0 0.0 reduce-scatter.2.cloned.1.call-done
Async XLA Ops:
  7.2 251.8 %reduce-scatter.2.cloned.1.call-start = ((), (), s32[]{:S(2)}) async-start(), calls=%async_computation.1 | async-start | bytes 18874368 | tf_op jit(solution)/shard_map/reduce_scatter | solution.py:441
Sparse Core Ops, SparseCore 0:
  154.6 88.6 reduce-scatter.1

commit v2 on v1

--- a/solution.py
+++ b/solution.py
@@ -12,6 +12,7 @@
 TN = (((0,), (0,)), ((), ()))
 VMEM_LIMIT = 67043328
 TILE = 1024
+PART = 256
 
 
 def dot(a, b, dims):
@@ -49,9 +50,12 @@
     def remote(which, k):
         mine, whole = ((dy, dy_all), (x, x_all))[which]
         device, h, own, target = plan[k]
+        landing = whole.at[span(device, h)]
+        if which == 0 and k in (4, 5):
+            landing = dy_tile.at[0, pl.ds(pl.multiple_of(core * rows + h * half, half), half)]
         return pltpu.make_async_remote_copy(
             src_ref=mine.at[pl.ds(h * half, half)] if own else whole.at[span(device, h)],
-            dst_ref=whole.at[span(device, h)],
+            dst_ref=landing,
             send_sem=send_sem.at[which, k],
             recv_sem=recv_sem.at[which, k],
             device_id={"tp": target},
@@ -115,13 +119,11 @@
 
     own_rows = pl.ds(pl.multiple_of(core * rows, rows), rows)
     all_rows = pl.ds(pl.multiple_of(me * rows, rows), rows)
+    chip_rows = pl.ds(pl.multiple_of(chip * 2 * rows, rows), 2 * rows)
     own_dy_in = pltpu.make_async_copy(dy, dy_tile.at[0, own_rows], own_sem.at[0])
-    own_dy_out = pltpu.make_async_copy(dy_tile.at[0, own_rows], dy_all.at[all_rows], own_sem.at[1])
+    chip_dy_out = pltpu.make_async_copy(dy_tile.at[0], dy_all.at[chip_rows], own_sem.at[1])
     own_x_in = pltpu.make_async_copy(x, x_own, own_sem.at[2])
     own_x_out = pltpu.make_async_copy(x_own, x_all.at[all_rows], own_sem.at[3])
-    partner_rows = pl.ds(pl.multiple_of((1 - core) * rows, rows), rows)
-    partner_all = pl.ds(pl.multiple_of(partner * rows, rows), rows)
-    partner_dy_in = pltpu.make_async_copy(dy_all.at[partner_all], dy_tile.at[0, partner_rows], own_sem.at[4])
 
     barrier = pltpu.get_barrier_semaphore()
     for target in (to_right, to_left, partner):
@@ -133,10 +135,8 @@
     load_act(0)
     own_x_in.start()
     own_dy_in.wait()
-    own_dy_out.start()
     arrived(0, 4, 5)
-    partner_dy_in.start()
-    partner_dy_in.wait()
+    chip_dy_out.start()
 
     def step(s, _):
         slot_dy = s % 2
@@ -168,14 +168,16 @@
                 pltpu.make_async_copy(grads, dy_all.at[pl.ds(0, 4 * half)], grads_sem).wait()
                 pltpu.make_async_copy(hid, hidden.at[pl.ds(0, 4 * half)], hid_sem).wait()
 
-            d_hidden = dot(dy_tile[slot_dy], w_tile[i], NT)
-            g, u = act_tile[i, :, :TILE].astype(F32), act_tile[i, :, TILE:].astype(F32)
-            sig = jax.nn.sigmoid(g)
-            act = g * sig
-            at = pl.multiple_of(i * TILE, TILE)
-            grads[:, pl.ds(at, TILE)] = (d_hidden * u * (sig + act * (1.0 - sig))).astype(BF16)
-            grads[:, pl.ds(ff + at, TILE)] = (d_hidden * act).astype(BF16)
-            hid[:, pl.ds(at, TILE)] = (act * u).astype(BF16)
+            for first in range(0, TILE, PART):
+                d_hidden = dot(dy_tile[slot_dy], w_tile[i, first : first + PART], NT)
+                g = act_tile[i, :, first : first + PART].astype(F32)
+                u = act_tile[i, :, TILE + first : TILE + first + PART].astype(F32)
+                sig = jax.nn.sigmoid(g)
+                act = g * sig
+                at = pl.multiple_of(i * TILE + first, PART)
+                grads[:, pl.ds(at, PART)] = (d_hidden * u * (sig + act * (1.0 - sig))).astype(BF16)
+                grads[:, pl.ds(ff + at, PART)] = (d_hidden * act).astype(BF16)
+                hid[:, pl.ds(at, PART)] = (act * u).astype(BF16)
             return 0
 
         lax.fori_loop(0, down_tiles, down, 0)
@@ -211,7 +213,7 @@
 
             @pl.when((s == 0) & (i == 3))
             def _():
-                own_dy_out.wait()
+                chip_dy_out.wait()
                 arrived(0, 8, 9)
 
             @pl.when((s == 1) & (i == 1))
@@ -319,7 +321,7 @@
             pltpu.VMEM((rows, width), BF16),
             pltpu.VMEM((group, TILE), BF16),
             pltpu.VMEM((2, group, TILE), BF16),
-            sem((2, 14)), sem((2, 14)), sem((2,)), sem((2,)), sem((2,)), sem, sem, sem((2,)), sem((5,)), sem((4,)),
+            sem((2, 14)), sem((2, 14)), sem((2,)), sem((2,)), sem((2,)), sem, sem, sem((2,)), sem((4,)), sem((4,)),
         ],
         compiler_params=pltpu.CompilerParams(collective_id=0, has_side_effects=True, vmem_limit_bytes=VMEM_LIMIT),
         cost_estimate=pl.CostEstimate(flops=6 * group * width * ff, bytes_accessed=16 * group * width, transcendentals=0),

time: 266 us -> 267 us (level)
  no operation moved by 1% of the time
where the time goes in v2:
time: 267 us
  Pallas kernels  253 us (95%)
  between operations  14.1 us (5%)
    pallas_call x1, Pallas kernels, gather_and_back(): pl.pallas_call(functools.partial(gather_kernel, n // 2), out_shape=[wide,...  148 us
    pallas_call x1, Pallas kernels, weight_grads(): pl.pallas_call(grads_kernel, in_specs=[any_] * 6, out_specs=[any_] * 3, o...  104 us
  transfers between devices with their start and end apart: 1, of which 0 were waited for; matrix products, arithmetic and copies ran while one was open for 0% of the time, Pallas kernels for 39%

profile of v2, /device:TPU:113, one launch (start us, length us, event | category | flops | bytes accessed | tf_op | source)
XLA Modules:
  0.0 266.9 jit_solution(2334773128374563929)
XLA Ops:
  7.2 0.1 reduce-scatter.2.cloned.1.call-start
  7.2 148.2 %gather_and_back.1 = (bf16[2048,4096]{1,0:T(8,128)(2,1)}, bf16[2048,4096]{1,0:T(8,128)(2,1)}, bf16[2048,2048]{1,0:T(8,128)(2,1)}, bf16[2048,2048]{1,0:T(8,128)(2...) custom-call(bf16[256,4096]{1,0:T(8,128)(2,1)} %dy.1, ...), custom_call_target="tpu_custom_call" | custom-call | flops 103079215104 | bytes 134217728 | tf_op jit(solution)/shard_map/gather_and_back/pallas_call | solution.py:309
  155.5 0.1 reduce-scatter.2.cloned.1.call-update
  155.5 104.4 %weight_grads.1 = (bf16[4096,2048]{1,0:T(8,128)(2,1)}, bf16[4096,2048]{1,0:T(8,128)(2,1)}, bf16[2048,4096]{1,0:T(8,128)(2,1)}) custom-call(bf16[2048,4096]{1,0:T(8,128)(2,1)} %get-tuple-element.15.x, bf16[2048,2048]{1,0:T(8,128)(2,1)} %get-tuple-element.16.d_gate, bf16[2048,2048]{1,0:T(8,128)(2,1)} %get-tuple-element.17.d_up, ...), custom_call_target="tpu_custom_call" | custom-call | flops 103079215104 | bytes 134217728 | tf_op jit(solution)/shard_map/weight_grads/pallas_call | solution.py:416
  260.0 0.0 reduce-scatter.2.cloned.1.call-done
Async XLA Ops:
  7.2 252.8 %reduce-scatter.2.cloned.1.call-start = ((), (), s32[]{:S(2)}) async-start(), calls=%async_computation.1 | async-start | bytes 18874368 | tf_op jit(solution)/shard_map/reduce_scatter | solution.py:443
Sparse Core Ops, SparseCore 0:
  155.6 87.6 reduce-scatter.1
